TPU v7x, 128 devices: a whole 4x4x4 slice. The times are simulated.
128 devices in a mesh: member: 8 (over x, core), region: 16 (over z, y).
Axes of the slice: x: 4, y: 4, z: 4, core: 2. Of those that a mesh axis runs over, the one named last changes fastest.
Arguments:
- ensemble: float32 [24, 32, 128, 512], P('member', 'region'), may hold values from -6 to 6
- obs_value: float32 [32, 128, 128], P(None, ('member', 'region')), may hold values from -6 to 6
- obs_error: float32 [32, 128, 128], P(None, ('member', 'region')), may hold values from 0.5 to 4
- obs_index: int32 [32, 128, 128], P(None, ('member', 'region')), may hold values from 0 to 511
- obs_count: int32 [32, 128], P(None, ('member', 'region')), may hold values from 1 to 128
Outputs:
- analysis: float32 [24, 32, 128, 512], P('member', 'region')
Inputs may be any that keep to these rules, and one draw needn't show every extreme that they name: `obs_index`: value v names field v // (256) (0 SST, 1 SSH) at cell v mod (256) of the block, cells row-major. `obs_count`: slots below a block's count are observations; the others are padding and carry no weight.
All inputs are finite; a program needn't handle non-finite values.
Results may differ from a plain program's by a relative error of at most 0.0001.
Values sent between devices are 32-bit elements; how exact they have to be, the bound alone decides.
No kernel may reach another device: no remote copies, remote signals or barrier semaphores. Data moves between devices by JAX's collectives and lax.ppermute only.
A program may use at most 64 MiB of HBM per device.

v0:
```python
import math

import jax
import jax.numpy as jnp
from jax import lax
from jax.sharding import PartitionSpec as P

SIDE = 16
NS_ITERS = 6


LOC_SCALE = 12.0
INFLATION_FACTOR = 1.1


def cut_along(shard, dim, devices):
    shape = shard.shape
    blocks = shard.reshape(*shape[:dim], devices, shape[dim] // devices, *shape[dim + 1 :])
    return jnp.moveaxis(blocks, dim, 0)


def laid_out(blocks, dim):
    blocks = jnp.moveaxis(blocks, 0, dim)
    shape = blocks.shape
    return blocks.reshape(*shape[:dim], shape[dim] * shape[dim + 1], *shape[dim + 2 :])


def exchange_both(shard, axis, axes, splits, concats):
    sizes = [lax.axis_size(a) for a in axes]
    blocks = cut_along(shard, splits[0], sizes[0])
    blocks = jnp.moveaxis(cut_along(blocks, splits[1] + 1, sizes[1]), 0, 1)
    inside = blocks.shape[2:]
    blocks = blocks.reshape(-1, *inside)
    blocks = lax.all_to_all(blocks, axis, split_axis=0, concat_axis=0, tiled=True)
    blocks = laid_out(blocks.reshape(*sizes, *inside), concats[0] + 1)
    return laid_out(blocks, concats[1])


def padded_2(shard, sides, width):
    edges = {}
    for axis, dim in sides:
        devices, length = (lax.axis_size(axis), shard.shape[dim])
        up = [(i, (i + 1) % devices) for i in range(devices - 1)]
        last = lax.slice_in_dim(shard, length - width, length, axis=dim)
        first = lax.slice_in_dim(shard, 0, width, axis=dim)
        edges[dim] = (
            lax.ppermute(last, axis, up),
            lax.ppermute(first, axis, [(b, a) for a, b in up]),
        )
    done = []
    for _, dim in sides:
        low, high = edges[dim]
        around = [(width, width) if d in done else (0, 0) for d in range(shard.ndim)]
        shard = jnp.concatenate([jnp.pad(low, around), shard, jnp.pad(high, around)], axis=dim)
        done.append(dim)
    return shard


def batch_product(left, right):
    return jnp.einsum("...ij,...jk->...ik", left, right, precision=lax.Precision.HIGHEST)


def observe(ensemble, obs_value, obs_error, obs_index, obs_count):
    ens_mean = jnp.mean(ensemble, axis=0)
    anomaly = ensemble - ens_mean
    slot_index = lax.broadcasted_iota(jnp.int32, obs_index.shape, 2)
    live_slot = jnp.where(slot_index < obs_count[:, :, None], 1.0, 0.0).astype(jnp.float32)
    root_weight = jnp.sqrt(live_slot / obs_error)
    value_count = anomaly.shape[3]
    value_ids = lax.broadcasted_iota(jnp.int32, (1, 1, 1, value_count), 3)
    selector = jnp.where(obs_index[:, :, :, None] == value_ids, 1.0, 0.0).astype(jnp.float32)
    seen_anom = jnp.einsum("rcov,krcv->rcko", selector, anomaly, precision=lax.Precision.HIGHEST)
    seen_mean = jnp.einsum("rcov,rcv->rco", selector, ens_mean, precision=lax.Precision.HIGHEST)
    rescaled_values = root_weight[:, :, None] * seen_anom
    innovation = root_weight * (obs_value - seen_mean)
    cell_index = obs_index % (SIDE * SIDE)
    rowpos = (cell_index // SIDE).astype(jnp.float32)
    column_position = (cell_index % SIDE).astype(jnp.float32)
    stacked = jnp.concatenate(
        [rescaled_values, innovation[:, :, None], rowpos[:, :, None], column_position[:, :, None]],
        axis=2,
    )
    return (anomaly, ens_mean, stacked)


def analyze(anomaly, ens_mean, padded):
    ensemble_members = anomaly.shape[0]
    row_count = anomaly.shape[1]
    col_count = anomaly.shape[2]
    pieces = []
    for row_step in range(3):
        for col_step in range(3):
            pieces.append(padded[row_step : row_step + row_count, col_step : col_step + col_count])
    nearby = jnp.stack(pieces, axis=2)
    rescaled_values = nearby[:, :, :, :ensemble_members]
    innovation = nearby[:, :, :, ensemble_members]
    rowpos = nearby[:, :, :, ensemble_members + 1]
    column_position = nearby[:, :, :, ensemble_members + 2]
    offset_index = jnp.arange(9, dtype=jnp.int32)
    offset_row = (offset_index // 3 - 1).astype(jnp.float32) * SIDE
    offset_col = (offset_index % 3 - 1).astype(jnp.float32) * SIDE
    half_side = SIDE // 2
    point_index = jnp.arange(4, dtype=jnp.int32)
    center_row = (point_index // 2).astype(jnp.float32) * half_side + (half_side - 1) * 0.5
    center_col = (point_index % 2).astype(jnp.float32) * half_side + (half_side - 1) * 0.5
    row_gap = offset_row[:, None] + rowpos
    col_gap = offset_col[:, None] + column_position
    distance = (row_gap[:, :, None] - center_row[:, None, None]) ** 2 + (
        col_gap[:, :, None] - center_col[:, None, None]
    ) ** 2
    locality = jnp.exp(-distance / (2.0 * LOC_SCALE * LOC_SCALE))
    weighted = locality[:, :, :, :, None, :] * rescaled_values[:, :, None]
    gramian_total = jnp.einsum(
        "rcpnko,rcnjo->rcpkj", weighted, rescaled_values, precision=lax.Precision.HIGHEST
    )
    drive_vec = jnp.einsum(
        "rcpnko,rcno->rcpk", weighted, innovation, precision=lax.Precision.HIGHEST
    )
    identity_matrix = jnp.eye(ensemble_members, dtype=jnp.float32)
    precision_matrix = gramian_total + (ensemble_members - 1) / INFLATION_FACTOR * identity_matrix
    norm_scale = jnp.sqrt(jnp.sum(precision_matrix * precision_matrix, axis=(3, 4), keepdims=True))
    root_iter = precision_matrix / norm_scale
    inv_iter = jnp.broadcast_to(identity_matrix, precision_matrix.shape)
    for sweep_index in range(NS_ITERS):
        ns_step = 1.5 * identity_matrix - 0.5 * batch_product(inv_iter, root_iter)
        root_iter = batch_product(root_iter, ns_step)
        inv_iter = batch_product(ns_step, inv_iter)
    inv_root = inv_iter / jnp.sqrt(norm_scale)
    half_way = jnp.einsum("rcpkj,rcpj->rcpk", inv_root, drive_vec, precision=lax.Precision.HIGHEST)
    mean_w = jnp.einsum("rcpkj,rcpj->rcpk", inv_root, half_way, precision=lax.Precision.HIGHEST)
    weights = mean_w[..., :, None] + math.sqrt(ensemble_members - 1) * inv_root
    point_weights = weights.reshape(row_count, col_count, 2, 2, ensemble_members, ensemble_members)
    shaped = anomaly.reshape(ensemble_members, row_count, col_count, 2, 2, half_side, 2, half_side)
    updated = jnp.einsum(
        "jrcvaybx,rcabjk->krcvaybx", shaped, point_weights, precision=lax.Precision.HIGHEST
    )
    return ens_mean[None] + updated.reshape(anomaly.shape)


def local(ensemble, obs_value, obs_error, obs_index, obs_count):
    by_block = exchange_both(ensemble, ("member", "region"), ("member", "region"), (2, 2), (0, 1))
    anomaly, ens_mean, stacked = observe(by_block, obs_value, obs_error, obs_index, obs_count)
    with_halo = padded_2(stacked, ((("member", "region"), 1),), 1)
    padded = jnp.pad(with_halo, ((1, 1), (0, 0), (0, 0), (0, 0)))
    row_span = anomaly.shape[1] // 8

    def one_group(turn_index, result):
        first_row_index = turn_index * row_span
        part_anom = lax.dynamic_slice_in_dim(anomaly, first_row_index, row_span, 1)
        part_mean = lax.dynamic_slice_in_dim(ens_mean, first_row_index, row_span, 0)
        part_pad = lax.dynamic_slice_in_dim(padded, first_row_index, row_span + 2, 0)
        return lax.dynamic_update_slice_in_dim(
            result, analyze(part_anom, part_mean, part_pad), first_row_index, 1
        )

    result = lax.fori_loop(0, 8, one_group, jnp.zeros_like(anomaly))
    by_rows = lax.all_to_all(result, "region", split_axis=1, concat_axis=2, tiled=True)
    return lax.all_to_all(by_rows, "member", split_axis=0, concat_axis=2, tiled=True)


def solution(mesh):
    return jax.shard_map(
        local,
        mesh=mesh,
        in_specs=(
            P("member", "region", None, None),
            P(None, ("member", "region"), None),
            P(None, ("member", "region"), None),
            P(None, ("member", "region"), None),
            P(None, ("member", "region")),
        ),
        out_specs=P("member", "region", None, None),
        check_vma=False,
    )
```

profile of v0, /device:TPU:1, one launch (start us, length us, event | category | flops | bytes accessed | tf_op | source)
XLA Modules:
  0.0 295.5 jit_solution(3947123815600746661)
XLA Ops:
  0.0 3.8 %copy.142 = f32[3,2,8,16,512]{4,1,0,3,2:T(2,128)} copy(f32[3,2,8,16,512]{4,3,2,1,0:T(8,128)} %bitcast.309) | data formatting | bytes 3145728 | tf_op jit(solution)/shard_map/reshape | solution.py:18
  3.8 11.5 %all-to-all-start = ((f32[128,3,2,1,512]{4,2,1,3,0:T(2,128)}), f32[128,3,2,1,512]{4,2,1,3,0:T(2,128)S(1)}, u32[]{:S(2)}, u32[]{:S(2)}) async-start(f32[128,3,2,1,512]{4,2,1,3,0:T(2,128)} %bitcast.48), calls=%async_computation | async-start | bytes 3145728 | tf_op jit(solution)/shard_map/all_to_all | solution.py:34
  15.3 23.9 %all-to-all-done = f32[128,3,2,1,512]{4,2,1,3,0:T(2,128)S(1)} async-done(((f32[128,3,2,1,512]{4,2,1,3,0:T(2,128)}), f32[128,3,2,1,512]{4,2,1,3,0:T(2,128)S(1)}, u32[]{:S(2)}, u32[]{:S(2)}) %all-to-all-start) | async-done | bytes 1572896 | tf_op jit(solution)/shard_map/all_to_all | solution.py:34
  41.3 7.9 %fusion.55 = f32[32,1,128]{2,1,0:T(1,128)S(1)} fusion(f32[32,512,1]{1,2,0:T(1,128)S(1)} %reshape.530, s32[32,128]{1,0:T(8,128)S(1)} %bitcast.321), kind=kOutput, calls=%fused_computation.91 | convolution fusion | flops 29360128 | bytes 98304 | tf_op jit(solution)/shard_map/rcov,rcv->rco/dot_general | solution.py:73
  49.3 7.8 %fusion.69 = f32[32,1,24,128]{3,2,0,1:T(8,128)S(1)} fusion(f32[24,32,512]{2,0,1:T(8,128)S(1)} %bitcast_subtract_fusion, s32[32,128]{1,0:T(8,128)S(1)} %bitcast.322, f32[32,128]{1,0:T(8,128)S(1)} %get-tuple-element.210), kind=kOutput, calls=%fused_computation.112 | convolution fusion | flops 608272384 | bytes 1998848 | tf_op jit(solution)/shard_map/rcov,krcv->rcko/dot_general | solution.py:72
  57.2 2.9 collective-permute-start
  60.1 6.0 %collective-permute-start.1 = (f32[32,1,27,128]{3,2,0,1:T(8,128)S(1)}, f32[32,1,27,128]{3,2,0,1:T(8,128)}, u32[]{:S(2)}, u32[]{:S(2)}) collective-permute-start(f32[32,1,27,128]{3,2,0,1:T(8,128)S(1)} %pad_maximum_fusion), channel_id=1, source_target_pairs={{1,0},{2,1},{3,2},{4,3},{5,4},{6,5},{7,6},{8,7},{9,8},{10,9},{11,1... | collective-permute-start | bytes 1327112 | tf_op jit(solution)/shard_map/ppermute | solution.py:48
  66.2 1.3 broadcast_subtract_fusion
  67.5 3.5 %collective-permute-done = f32[32,1,27,128]{3,2,0,1:T(8,128)S(1)} collective-permute-done((f32[32,1,27,128]{3,2,0,1:T(8,128)S(1)}, f32[32,1,27,128]{3,2,0,1:T(8,128)S(1)}, u32[]{:S(2)}, u32[]{:S(2)}) %collective-permute-start) | collective-permute-done | bytes 442400 | tf_op jit(solution)/shard_map/ppermute | solution.py:47
  71.1 6.8 %collective-permute-done.1 = f32[32,1,27,128]{3,2,0,1:T(8,128)} collective-permute-done((f32[32,1,27,128]{3,2,0,1:T(8,128)S(1)}, f32[32,1,27,128]{3,2,0,1:T(8,128)}, u32[]{:S(2)}, u32[]{:S(2)}) %collective-permute-start.1) | collective-permute-done | bytes 442400 | tf_op jit(solution)/shard_map/ppermute | solution.py:48
  77.9 1.2 select_maximum_fusion
  79.1 1.3 broadcast_in_dim.83.clone
  80.4 159.7 %while.16 = (s32[]{:T(128)}, f32[24,32,1,512]{3,0,2,1:T(8,128)}, f32[32,1,512]{2,0,1:T(8,128)S(1)}, f32[34,3,27,128]{3,2,0,1:T(8,128)S(1)}, f32[24,32,1,512]{3,0...) while((s32[]{:T(128)}, f32[24,32,1,512]{3,0,2,1:T(8,128)}, ...), condition=%wide.region_3.4_spmd, body=%wide.region_1.3_spmd.sunk | while | flops 193469024 | bytes 8862404 | solution.py:156
  81.1 4.9 %fusion.273 = f32[4,4,24,1]{2,3,1,0:T(1,128)S(1)} fusion(f32[4,9,24,128]{3,2,1,0:T(8,128)S(1)} %slice_bitcast_fusion.2, f32[4,4,9,128]{3,2,1,0:T(8,128)S(1)} %multiply_exponential_fusion.2, f32[4,9,128,1,1]{2,0,1,3,4:T(4,128)S(1)} %bitcast.311), kind=kOutput, calls=%fused_computation.21.clone.1 | convolution fusion | flops 5750784 | bytes 536064 | tf_op jit(solution)/shard_map/while/body/eval_jaxpr/rcpnko,rcno->rcpk/dot_general | solution.py:116
  86.0 1.8 multiply_reduce_fusion.2
  96.7 0.9 constant_dynamic-slice_fusion.2
  98.0 1.0 convolution_bitcast_fusion.5
  101.0 4.9 %fusion.273 = f32[4,4,24,1]{2,3,1,0:T(1,128)S(1)} fusion(f32[4,9,24,128]{3,2,1,0:T(8,128)S(1)} %slice_bitcast_fusion.2, f32[4,4,9,128]{3,2,1,0:T(8,128)S(1)} %multiply_exponential_fusion.2, f32[4,9,128,1,1]{2,0,1,3,4:T(4,128)S(1)} %bitcast.311), kind=kOutput, calls=%fused_computation.21.clone.1 | convolution fusion | flops 5750784 | bytes 536064 | tf_op jit(solution)/shard_map/while/body/eval_jaxpr/rcpnko,rcno->rcpk/dot_general | solution.py:116
  106.0 1.8 multiply_reduce_fusion.2
  116.7 0.9 constant_dynamic-slice_fusion.2
  118.0 1.0 convolution_bitcast_fusion.5
  121.0 4.9 %fusion.273 = f32[4,4,24,1]{2,3,1,0:T(1,128)S(1)} fusion(f32[4,9,24,128]{3,2,1,0:T(8,128)S(1)} %slice_bitcast_fusion.2, f32[4,4,9,128]{3,2,1,0:T(8,128)S(1)} %multiply_exponential_fusion.2, f32[4,9,128,1,1]{2,0,1,3,4:T(4,128)S(1)} %bitcast.311), kind=kOutput, calls=%fused_computation.21.clone.1 | convolution fusion | flops 5750784 | bytes 536064 | tf_op jit(solution)/shard_map/while/body/eval_jaxpr/rcpnko,rcno->rcpk/dot_general | solution.py:116
  125.9 1.8 multiply_reduce_fusion.2
  136.6 0.9 constant_dynamic-slice_fusion.2
  137.9 1.0 convolution_bitcast_fusion.5
  141.0 4.9 %fusion.273 = f32[4,4,24,1]{2,3,1,0:T(1,128)S(1)} fusion(f32[4,9,24,128]{3,2,1,0:T(8,128)S(1)} %slice_bitcast_fusion.2, f32[4,4,9,128]{3,2,1,0:T(8,128)S(1)} %multiply_exponential_fusion.2, f32[4,9,128,1,1]{2,0,1,3,4:T(4,128)S(1)} %bitcast.311), kind=kOutput, calls=%fused_computation.21.clone.1 | convolution fusion | flops 5750784 | bytes 536064 | tf_op jit(solution)/shard_map/while/body/eval_jaxpr/rcpnko,rcno->rcpk/dot_general | solution.py:116
  145.9 1.8 multiply_reduce_fusion.2
  156.6 0.9 constant_dynamic-slice_fusion.2
  157.9 1.0 convolution_bitcast_fusion.5
  160.9 4.9 %fusion.273 = f32[4,4,24,1]{2,3,1,0:T(1,128)S(1)} fusion(f32[4,9,24,128]{3,2,1,0:T(8,128)S(1)} %slice_bitcast_fusion.2, f32[4,4,9,128]{3,2,1,0:T(8,128)S(1)} %multiply_exponential_fusion.2, f32[4,9,128,1,1]{2,0,1,3,4:T(4,128)S(1)} %bitcast.311), kind=kOutput, calls=%fused_computation.21.clone.1 | convolution fusion | flops 5750784 | bytes 536064 | tf_op jit(solution)/shard_map/while/body/eval_jaxpr/rcpnko,rcno->rcpk/dot_general | solution.py:116
  165.9 1.8 multiply_reduce_fusion.2
  176.6 0.9 constant_dynamic-slice_fusion.2
  177.9 1.0 convolution_bitcast_fusion.5
  180.9 4.9 %fusion.273 = f32[4,4,24,1]{2,3,1,0:T(1,128)S(1)} fusion(f32[4,9,24,128]{3,2,1,0:T(8,128)S(1)} %slice_bitcast_fusion.2, f32[4,4,9,128]{3,2,1,0:T(8,128)S(1)} %multiply_exponential_fusion.2, f32[4,9,128,1,1]{2,0,1,3,4:T(4,128)S(1)} %bitcast.311), kind=kOutput, calls=%fused_computation.21.clone.1 | convolution fusion | flops 5750784 | bytes 536064 | tf_op jit(solution)/shard_map/while/body/eval_jaxpr/rcpnko,rcno->rcpk/dot_general | solution.py:116
  185.8 1.8 multiply_reduce_fusion.2
  196.5 0.9 constant_dynamic-slice_fusion.2
  197.8 1.0 convolution_bitcast_fusion.5
  200.9 4.9 %fusion.273 = f32[4,4,24,1]{2,3,1,0:T(1,128)S(1)} fusion(f32[4,9,24,128]{3,2,1,0:T(8,128)S(1)} %slice_bitcast_fusion.2, f32[4,4,9,128]{3,2,1,0:T(8,128)S(1)} %multiply_exponential_fusion.2, f32[4,9,128,1,1]{2,0,1,3,4:T(4,128)S(1)} %bitcast.311), kind=kOutput, calls=%fused_computation.21.clone.1 | convolution fusion | flops 5750784 | bytes 536064 | tf_op jit(solution)/shard_map/while/body/eval_jaxpr/rcpnko,rcno->rcpk/dot_general | solution.py:116
  205.8 1.8 multiply_reduce_fusion.2
  217.8 1.0 convolution_bitcast_fusion.5
  220.8 4.9 %fusion.273 = f32[4,4,24,1]{2,3,1,0:T(1,128)S(1)} fusion(f32[4,9,24,128]{3,2,1,0:T(8,128)S(1)} %slice_bitcast_fusion.2, f32[4,4,9,128]{3,2,1,0:T(8,128)S(1)} %multiply_exponential_fusion.2, f32[4,9,128,1,1]{2,0,1,3,4:T(4,128)S(1)} %bitcast.311), kind=kOutput, calls=%fused_computation.21.clone.1 | convolution fusion | flops 5750784 | bytes 536064 | tf_op jit(solution)/shard_map/while/body/eval_jaxpr/rcpnko,rcno->rcpk/dot_general | solution.py:116
  225.8 1.8 multiply_reduce_fusion.2
  236.5 0.9 constant_dynamic-slice_fusion.2
  237.8 1.0 convolution_bitcast_fusion.5
  240.2 23.2 %all_to_all.41 = f32[24,32,1,512]{3,0,2,1:T(8,128)S(1)} all-to-all(f32[24,32,1,512]{3,0,2,1:T(8,128)} %get-tuple-element.173), channel_id=1, replica_groups=mesh['member'=8,'region'=16] {'region'}, dimensions={1} | all-to-all | bytes 3145728 | tf_op jit(solution)/shard_map/all_to_all | solution.py:157
  263.4 1.2 copy.157
  264.6 29.3 %all_to_all.42 = f32[24,2,16,512]{3,1,2,0:T(2,128)S(1)} all-to-all(f32[24,2,16,512]{3,1,2,0:T(2,128)S(1)} %copy.157), channel_id=1, replica_groups=mesh['member'=8,'region'=16] {'member'}, dimensions={0} | all-to-all | bytes 3145728 | tf_op jit(solution)/shard_map/all_to_all | solution.py:158
  294.2 1.4 copy.159
  (415 shorter events, 91.5 us)
Async XLA Ops:
  3.8 11.5 %copy-start.2 = (s32[32,1,128]{2,1,0:T(1,128)S(1)}, s32[32,1,128]{2,1,0:T(1,128)}, u32[]{:S(2)}) copy-start(s32[32,1,128]{2,1,0:T(1,128)} %param.10) | copy-start | bytes 49156
  3.8 35.5 %all-to-all-start = ((f32[128,3,2,1,512]{4,2,1,3,0:T(2,128)}), f32[128,3,2,1,512]{4,2,1,3,0:T(2,128)S(1)}, u32[]{:S(2)}, u32[]{:S(2)}) async-start(f32[128,3,2,1,512]{4,2,1,3,0:T(2,128)} %bitcast.48), calls=%async_computation | async-start | bytes 3145728 | tf_op jit(solution)/shard_map/all_to_all | solution.py:34
  41.2 8.0 %copy-start = (f32[32,1,128]{2,1,0:T(1,128)S(1)}, f32[32,1,128]{2,1,0:T(1,128)}, u32[]{:S(2)}) copy-start(f32[32,1,128]{2,1,0:T(1,128)} %param.9) | copy-start | bytes 49156
  41.2 8.0 %copy-start.1 = (f32[32,1,128]{2,1,0:T(1,128)S(1)}, f32[32,1,128]{2,1,0:T(1,128)}, u32[]{:S(2)}) copy-start(f32[32,1,128]{2,1,0:T(1,128)} %param.8) | copy-start | bytes 49156
  41.2 8.0 %copy-start.3 = (s32[32,1]{0,1:T(1,128)S(1)}, s32[32,1]{0,1:T(1,128)}, u32[]{:S(2)}) copy-start(s32[32,1]{0,1:T(1,128)} %param.11) | copy-start | bytes 388
  57.2 13.8 %collective-permute-start = (f32[32,1,27,128]{3,2,0,1:T(8,128)S(1)}, f32[32,1,27,128]{3,2,0,1:T(8,128)S(1)}, u32[]{:S(2)}, u32[]{:S(2)}) collective-permute-start(f32[32,1,27,128]{3,2,0,1:T(8,128)S(1)} %pad_maximum_fusion), channel_id=1, source_target_pairs={{0,1},{1,2},{2,3},{3,4},{4,5},{5,6},{6,7},{7,8},{8,9},{9,10},{10,1... | collective-permute-start | bytes 1327112 | tf_op jit(solution)/shard_map/ppermute | solution.py:47
  60.1 17.7 %collective-permute-start.1 = (f32[32,1,27,128]{3,2,0,1:T(8,128)S(1)}, f32[32,1,27,128]{3,2,0,1:T(8,128)}, u32[]{:S(2)}, u32[]{:S(2)}) collective-permute-start(f32[32,1,27,128]{3,2,0,1:T(8,128)S(1)} %pad_maximum_fusion), channel_id=1, source_target_pairs={{1,0},{2,1},{3,2},{4,3},{5,4},{6,5},{7,6},{8,7},{9,8},{10,9},{11,1... | collective-permute-start | bytes 1327112 | tf_op jit(solution)/shard_map/ppermute | solution.py:48
where the time goes:
time: 296 us
  matrix products  146 us (49%)
  blocking collectives  52.4 us (18%)
  waiting for transfers between devices  34.2 us (12%)
  local copies, waits for them, and re-layouts  30.4 us (10%)
  starting transfers between devices  20.4 us (7%)
  other arithmetic  9.16 us (3%)
    dot_general x136, matrix products, batch_product(): jnp.einsum('...ij,...jk->...ik', left, right, precision=lax.Precision.HIG...  62 us
    dot_general x8, matrix products, analyze(): jnp.einsum('rcpnko,rcno->rcpk', weighted, innovation, precision=lax.Preci...  39.3 us
    all_to_all x1, blocking collectives, local(): lax.all_to_all(by_rows, 'member', split_axis=0, concat_axis=2, tiled=True)  29.3 us
    all_to_all x1, waiting for transfers between devices, exchange_both(): lax.all_to_all(blocks, axis, split_axis=0, concat_axis=0, tiled=True)  23.9 us
    all_to_all x1, blocking collectives, local(): lax.all_to_all(result, 'region', split_axis=1, concat_axis=2, tiled=True)  23.2 us
    dot_general x8, matrix products, analyze(): jnp.einsum('rcpnko,rcnjo->rcpkj', weighted, rescaled_values, precision=la...  14.5 us
    all_to_all x1, starting transfers between devices, exchange_both(): lax.all_to_all(blocks, axis, split_axis=0, concat_axis=0, tiled=True)  11.5 us
    dynamic_slice x16, local copies, waits for them, and re-layouts, one_group(): part_anom = lax.dynamic_slice_in_dim(anomaly, first_row_index, row_span, 1)  10.2 us
  transfers between devices with their start and end apart: 3, of which 3 were waited for; matrix products, arithmetic and copies ran while one was open for 0% of the time, Pallas kernels for 0%

commit v1 on v0

v1 whole, which is shorter than its diff:
```python
import math

import jax
import jax.numpy as jnp
from jax import lax
from jax.experimental import pallas as pl
from jax.experimental.pallas import tpu as pltpu
from jax.sharding import PartitionSpec as P

SIDE = 16
NS_ITERS = 6
MEMBERS = 24
OBS = 128
VALS = 512
INFLATION_FACTOR = 1.1
INV_SCALE = 1.0 / 288.0

ROWS = 2
COLS = 16
BLOCKS = ROWS * COLS
POINTS = 4
EXT_COLS = COLS + 2
EXT = (ROWS + 2) * EXT_COLS
SLAB = 32
STRIDE = BLOCKS * 4


def observe_kernel(ens_ref, obs_ref, out_ref):
    sub = lax.broadcasted_iota(jnp.int32, (8, OBS), 0)

    def body(c, carry):
        obs = obs_ref[c]
        for i in range(ROWS):
            value = obs[i : i + 1]
            weight = obs[2 + i : 3 + i]
            index_f = obs[4 + i : 5 + i]
            index = jnp.broadcast_to(index_f.astype(jnp.int32), (MEMBERS, OBS))
            lane = index & 127
            chunk = index >> 7
            first = (2 * i + (c >> 3)) * 32 + (c & 7)
            seen = jnp.zeros((MEMBERS, OBS), jnp.float32)
            for t in range(4):
                ens = ens_ref[pl.ds(first + 8 * t, MEMBERS, stride=STRIDE), :]
                got = jnp.take_along_axis(ens, lane, axis=1, mode="promise_in_bounds")
                seen = jnp.where(chunk == t, got, seen)
            mean = jnp.sum(seen, axis=0, keepdims=True) * (1.0 / MEMBERS)
            out_ref[i, c, 0:MEMBERS, :] = weight * (seen - mean)
            innovation = weight * (value - mean)
            out_ref[i, c, MEMBERS:SLAB, :] = jnp.where(
                sub == 0, innovation, jnp.where(sub == 1, index_f, 0.0)
            )
        return carry

    lax.fori_loop(0, COLS, body, 0)


def split_bf16(x):
    high = x.astype(jnp.bfloat16)
    low = (x - high.astype(jnp.float32)).astype(jnp.bfloat16)
    return high, low


def sym_product(left, right, out, finish):
    for tile in range(3):
        lo = 8 * tile
        for half in range(2):
            i0 = lo + 4 * half
            acc = None
            for k in range(MEMBERS):
                term = left[i0 : i0 + 4, k : k + 1, :] * right[k : k + 1, lo:MEMBERS, :]
                acc = term if acc is None else acc + term
            for step in range(4):
                i = i0 + step
                row = finish(acc[step], i, lo)
                out[i, lo:MEMBERS, :] = row
                for j in range(tile + 1, 3):
                    out[8 * j : 8 * j + 8, i, :] = row[8 * (j - tile) : 8 * (j - tile) + 8]


def plain(row, i, lo):
    return row


def newton_step(row, i, lo):
    where = lax.broadcasted_iota(jnp.int32, row.shape, 0) + lo
    return jnp.where(where == i, 1.5, 0.0) - 0.5 * row


def analyze_kernel(
    ens_ref, own_ref, top_ref, bot_ref, left_ref, right_ref, out_ref,
    source, pair, locs, gram, ya, yb, za, zb, mm, drive,
):
    t = lax.broadcasted_iota(jnp.int32, (8, OBS), 0)
    offset = (((t >> 1) - 1) * SIDE - (t & 1) * 8).astype(jnp.float32) - 3.5

    def put(slot, slab):
        cell = slab[25:26].astype(jnp.int32) & 255
        dy = (cell >> 4).astype(jnp.float32) + offset
        dx = (cell & 15).astype(jnp.float32) + offset
        locs[slot, 0:8, :] = jnp.exp(-(dy * dy) * INV_SCALE)
        locs[slot, 8:16, :] = jnp.exp(-(dx * dx) * INV_SCALE)
        source[slot] = slab[0:MEMBERS]
        high, low = split_bf16(slab)
        pair[slot] = jnp.concatenate([high, low], axis=0)

    def put_column(c, carry):
        for i in range(ROWS):
            put((i + 1) * EXT_COLS + 1 + c, own_ref[i, c])
        return carry

    def put_edge(c, carry):
        put(c, top_ref[c])
        put((ROWS + 1) * EXT_COLS + c, bot_ref[c])
        return carry

    lax.fori_loop(0, COLS, put_column, 0)
    lax.fori_loop(0, EXT_COLS, put_edge, 0)
    for i in range(ROWS):
        put((i + 1) * EXT_COLS, left_ref[i, 0])
        put((i + 1) * EXT_COLS + EXT_COLS - 1, right_ref[i, 0])

    def one_gram(c, carry):
        for i in range(ROWS):
            acc = jnp.zeros((POINTS * MEMBERS, 2 * SLAB), jnp.float32)
            for di in range(3):
                for dj in range(3):
                    slot = (i + di) * EXT_COLS + c + dj
                    loc = locs[slot]
                    base = source[slot]
                    rows = []
                    for a in range(2):
                        for b in range(2):
                            w = loc[2 * di + a : 2 * di + a + 1] * loc[8 + 2 * dj + b : 9 + 2 * dj + b]
                            rows.append(w * base)
                    high, low = split_bf16(jnp.concatenate(rows, axis=0))
                    both = pair[slot]
                    acc = acc + lax.dot_general(
                        jnp.concatenate([high, low], axis=1),
                        jnp.concatenate([both, both], axis=1),
                        (((1,), (1,)), ((), ())),
                        preferred_element_type=jnp.float32,
                    )
            start = pl.multiple_of((i * COLS + c) * (POINTS * MEMBERS), 8)
            gram[pl.ds(start, POINTS * MEMBERS), 0 : 2 * SLAB] = acc
        return carry

    lax.fori_loop(0, COLS, one_gram, 0)

    member = lax.broadcasted_iota(jnp.int32, (MEMBERS, 128), 0)
    squares = jnp.zeros((MEMBERS, 128), jnp.float32)
    for k in range(MEMBERS):
        turned = gram[pl.ds(k, 128, stride=MEMBERS), :].T
        total = turned[0:SLAB] + turned[SLAB : 2 * SLAB]
        row = total[0:MEMBERS] + jnp.where(member == k, (MEMBERS - 1) / INFLATION_FACTOR, 0.0)
        drive[k : k + 1, :] = total[MEMBERS : MEMBERS + 1]
        ya[k] = row
        squares = squares + row * row
    norm = jnp.sqrt(jnp.sum(squares, axis=0, keepdims=True))
    inverse = 1.0 / norm
    for k in range(MEMBERS):
        row = ya[k] * inverse
        ya[k] = row
        za[k] = newton_step(row, k, 0)

    sym_product(ya, za, yb, plain)

    def two_steps(turn, carry):
        sym_product(za, yb, mm, newton_step)
        sym_product(yb, mm, ya, plain)
        sym_product(mm, za, zb, plain)
        sym_product(zb, ya, mm, newton_step)
        sym_product(ya, mm, yb, plain)
        sym_product(mm, zb, za, plain)
        return carry

    lax.fori_loop(0, (NS_ITERS - 2) // 2, two_steps, 0)
    sym_product(za, yb, mm, newton_step)
    sym_product(mm, za, zb, plain)

    scale = 1.0 / jnp.sqrt(norm)
    half_way = jnp.zeros((MEMBERS, 128), jnp.float32)
    for k in range(MEMBERS):
        half_way = half_way + zb[k] * drive[k : k + 1, :]
    half_way = half_way * scale
    mean_w = jnp.zeros((MEMBERS, 128), jnp.float32)
    for k in range(MEMBERS):
        mean_w = mean_w + zb[k] * half_way[k : k + 1]
    mean_w = mean_w * scale
    spread = scale * math.sqrt(MEMBERS - 1)
    blank = jnp.zeros((128 - 3 * MEMBERS, 128), jnp.float32)
    for k in range(MEMBERS):
        weight = mean_w + spread * zb[k]
        high = weight.astype(jnp.bfloat16).astype(jnp.float32)
        gram[pl.ds(k, 128, stride=MEMBERS), :] = jnp.concatenate(
            [high, high, weight - high, blank], axis=0
        ).T

    right_half = (lax.broadcasted_iota(jnp.int32, (MEMBERS, 128), 1) >> 3) & 1

    def one_update(c, carry):
        for i in range(ROWS):
            block = i * COLS + c
            start = pl.multiple_of(block * (POINTS * MEMBERS), 8)
            weight = gram[pl.ds(start, POINTS * MEMBERS), :].astype(jnp.bfloat16)
            first = (2 * i + (c >> 3)) * 32 + (c & 7)
            ens = jnp.concatenate(
                [ens_ref[pl.ds(first + 8 * t, MEMBERS, stride=STRIDE), :] for t in range(4)], axis=1
            )
            mean = jnp.sum(ens, axis=0, keepdims=True) * (1.0 / MEMBERS)
            anomaly = ens - mean
            high = anomaly.astype(jnp.bfloat16).astype(jnp.float32)
            low = anomaly - high
            stacked = jnp.concatenate(
                [high, low, high, jnp.zeros((128 - 3 * MEMBERS, VALS), jnp.float32)], axis=0
            ).astype(jnp.bfloat16)
            for a in range(2):
                values = jnp.concatenate(
                    [stacked[:, 128 * a : 128 * a + 128], stacked[:, 256 + 128 * a : 384 + 128 * a]], axis=1
                )
                moved = jnp.dot(
                    weight[48 * a : 48 * a + 48], values, preferred_element_type=jnp.float32
                )
                for f in range(2):
                    part = moved[:, 128 * f : 128 * f + 128]
                    t = 2 * f + a
                    moved_tile = jnp.where(right_half == 1, part[MEMBERS:], part[:MEMBERS])
                    out_ref[pl.ds(first + 8 * t, MEMBERS, stride=STRIDE), :] = (
                        mean[:, 128 * t : 128 * t + 128] + moved_tile
                    )
        return carry

    lax.fori_loop(0, COLS, one_update, 0)


def vmem_call(kernel, shape, scratch=()):
    return pl.pallas_call(
        kernel,
        out_shape=jax.ShapeDtypeStruct(shape, jnp.float32),
        scratch_shapes=list(scratch),
        compiler_params=pltpu.CompilerParams(vmem_limit_bytes=40 * 1024 * 1024),
    )


def shifted(x, axis, by):
    devices = lax.axis_size(axis)
    pairs = [(i, i + by) for i in range(devices) if 0 <= i + by < devices]
    return lax.ppermute(x, axis, pairs)


def local(ensemble, obs_value, obs_error, obs_index, obs_count):
    tiled = ensemble.reshape(3, ROWS, 8, 2, 8, 4, 128).transpose(2, 0, 1, 3, 5, 4, 6)
    by_block = lax.all_to_all(tiled, "member", split_axis=0, concat_axis=0, tiled=True)
    by_block = by_block.reshape(MEMBERS * STRIDE, 128)

    slot = lax.broadcasted_iota(jnp.int32, (32, 1, OBS), 2)
    live = jnp.where(slot < obs_count[:, :, None], 1.0, 0.0).astype(jnp.float32)
    root_weight = jnp.sqrt(live / obs_error)
    pieces = [obs_value, root_weight, obs_index.astype(jnp.float32), jnp.zeros_like(obs_value)]
    packed = jnp.concatenate([x.reshape(COLS, ROWS, OBS) for x in pieces], axis=1)
    obs = lax.all_to_all(packed, "region", split_axis=0, concat_axis=0, tiled=True)

    own = vmem_call(observe_kernel, (ROWS, COLS, SLAB, OBS))(by_block, obs)

    left = shifted(own[:, COLS - 1 :], "member", 1)
    right = shifted(own[:, :1], "member", -1)
    top = shifted(jnp.concatenate([left[1], own[1], right[1]], axis=0), "region", 1)
    bot = shifted(jnp.concatenate([left[0], own[0], right[0]], axis=0), "region", -1)

    square = pltpu.VMEM((MEMBERS, MEMBERS, 128), jnp.float32)
    result = vmem_call(
        analyze_kernel,
        (MEMBERS * STRIDE, 128),
        (
            pltpu.VMEM((EXT, MEMBERS, OBS), jnp.float32),
            pltpu.VMEM((EXT, 2 * SLAB, OBS), jnp.bfloat16),
            pltpu.VMEM((EXT, 16, OBS), jnp.float32),
            pltpu.VMEM((BLOCKS * POINTS * MEMBERS, 128), jnp.float32),
            square, square, square, square, square,
            pltpu.VMEM((MEMBERS, 128), jnp.float32),
        ),
    )(by_block, own, top, bot, left, right)
    result = result.reshape(8, 3, ROWS, 2, 4, 8, 128)
    by_member = lax.all_to_all(result, "member", split_axis=0, concat_axis=0, tiled=True)
    return by_member.transpose(1, 2, 0, 3, 5, 4, 6).reshape(3, ROWS, 8 * COLS, VALS)


def solution(mesh):
    return jax.shard_map(
        local,
        mesh=mesh,
        in_specs=(
            P("member", "region", None, None),
            P(None, ("member", "region"), None),
            P(None, ("member", "region"), None),
            P(None, ("member", "region"), None),
            P(None, ("member", "region")),
        ),
        out_specs=P("member", "region", None, None),
        check_vma=False,
    )
```

time: 296 us -> 112 us (0.38)
  matrix products: 146 us -> 0 us
  local copies, waits for them, and re-layouts: 30.4 us -> 2.95 us
  Pallas kernels: 0 us -> 19.6 us
  waiting for transfers between devices: 34.2 us -> 16.2 us
  other arithmetic: 9.16 us -> 3.03 us
  starting transfers between devices: 20.4 us -> 17.3 us
    dot_general x178 -> x0, matrix products: 146 us -> none  [the longest x136 62 us: batch_product(): jnp.einsum('...ij,...jk->...ik', left, right, precision=lax.Precision.HIG...]
    pallas_call x0 -> x2, Pallas kernels: none -> 19.6 us  [the longest x1 17.3 us: local(): vmem_call(analyze_kernel, (MEMBERS * STRIDE, 128), (pltpu.VMEM((EXT, MEMB...]
    all_to_all x1, waiting for transfers between devices: 23.9 us -> 4.97 us  [local(): lax.all_to_all(packed, 'region', split_axis=0, concat_axis=0, tiled=True)]
    dynamic_slice x16 -> x0, local copies, waits for them, and re-layouts: 10.2 us -> none  [one_group(): part_anom = lax.dynamic_slice_in_dim(anomaly, first_row_index, row_span, 1)]
    dynamic_update_slice x16 -> x0, local copies, waits for them, and re-layouts: 8 us -> none  [one_group(): lax.dynamic_update_slice_in_dim(result, analyze(part_anom, part_mean, par...]
    add x40 -> x0, other arithmetic: 4.93 us -> none  [the longest x8 2.68 us: analyze(): return ens_mean[None] + updated.reshape(anomaly.shape)]
    all_to_all x4 -> x0, local copies, waits for them, and re-layouts: 3.15 us -> none  [the longest x2 1.64 us: local(): lax.all_to_all(by_rows, 'member', split_axis=0, concat_axis=2, tiled=True)]
    ppermute x2 -> x4, waiting for transfers between devices: 10.3 us -> 11.2 us  [shifted(): return lax.ppermute(x, axis, pairs)]
  transfers between devices with their start and end apart: 3 -> 5, of which waited for: 3 -> 4; matrix products, arithmetic and copies ran while one was open for 0% -> 1% of each run, Pallas kernels for 0% -> 0%
where the time goes in v1:
time: 112 us; the launch traced here: 110 us
  blocking collectives  50.9 us (45%)
  Pallas kernels  19.6 us (18%)
  starting transfers between devices  17.3 us (15%)
  waiting for transfers between devices  16.2 us (14%)
  other arithmetic  3.03 us (3%)
  local copies, waits for them, and re-layouts  2.95 us (3%)
    all_to_all x1, blocking collectives, local(): lax.all_to_all(tiled, 'member', split_axis=0, concat_axis=0, tiled=True)  26.7 us
    all_to_all x1, blocking collectives, local(): lax.all_to_all(result, 'member', split_axis=0, concat_axis=0, tiled=True)  24.1 us
    pallas_call x1, Pallas kernels, local(): vmem_call(analyze_kernel, (MEMBERS * STRIDE, 128), (pltpu.VMEM((EXT, MEMB...  17.3 us
    ppermute x4, waiting for transfers between devices, shifted(): return lax.ppermute(x, axis, pairs)  11.2 us
    ppermute x4, starting transfers between devices, shifted(): return lax.ppermute(x, axis, pairs)  8.69 us
    all_to_all x1, starting transfers between devices, local(): lax.all_to_all(packed, 'region', split_axis=0, concat_axis=0, tiled=True)  8.59 us
    all_to_all x1, waiting for transfers between devices, local(): lax.all_to_all(packed, 'region', split_axis=0, concat_axis=0, tiled=True)  4.97 us
    pallas_call x1, Pallas kernels, local(): own = vmem_call(observe_kernel, (ROWS, COLS, SLAB, OBS))(by_block, obs)  2.3 us
  transfers between devices with their start and end apart: 5, of which 4 were waited for; matrix products, arithmetic and copies ran while one was open for 1% of the time, Pallas kernels for 0%

profile of v1, /device:TPU:1, one launch (start us, length us, event | category | flops | bytes accessed | tf_op | source)
XLA Modules:
  0.0 110.0 jit_solution(6616051748391120526)
XLA Ops:
  0.0 0.7 convert_element_type.3
  0.7 0.1 pad.9.clone
  0.8 0.8 fusion.1
  1.7 1.4 %maximum_maximum_fusion = f32[16,8,128]{2,1,0:T(8,128)} fusion(f32[16,2,128]{2,1,0:T(2,128)S(1)} %bitcast.30, f32[16,2,128]{2,1,0:T(2,128)S(1)} %bitcast.31, f32[16,2,128]{2,1,0:T(2,128)} %bitcast.32, f32[8]{0:T(128)S(1)} %pad.9.clone), kind=kLoop, calls=%fused_computation.5 | loop fusion | flops 49152 | bytes 114720 | tf_op jit(solution)/shard_map/concatenate | solution.py:259
  3.1 8.6 %all-to-all-start.1 = ((f32[16,8,128]{2,1,0:T(8,128)}), f32[16,8,128]{2,1,0:T(8,128)S(1)}, u32[]{:S(2)}, u32[]{:S(2)}) async-start(f32[16,8,128]{2,1,0:T(8,128)} %maximum_maximum_fusion), calls=%async_computation.1 | async-start | bytes 131072 | tf_op jit(solution)/shard_map/all_to_all | solution.py:260
  11.7 1.5 %copy.9 = f32[3,2,8,2,8,4,128]{6,4,5,3,1,0,2:T(8,128)S(1)} copy(f32[3,2,8,2,8,4,128]{6,4,5,3,2,1,0:T(8,128)} %bitcast.29) | data formatting | bytes 3145728 | tf_op jit(solution)/shard_map/reshape | solution.py:251
  13.2 5.0 %all-to-all-done.1.obs_ref = f32[16,8,128]{2,1,0:T(8,128)S(1)} async-done(((f32[16,8,128]{2,1,0:T(8,128)}), f32[16,8,128]{2,1,0:T(8,128)S(1)}, u32[]{:S(2)}, u32[]{:S(2)}) %all-to-all-start.1) | async-done | bytes 65568 | tf_op jit(solution)/shard_map/all_to_all | solution.py:260
  18.2 26.7 %all_to_all.15 = f32[8,3,2,2,4,8,128]{6,5,4,3,2,1,0:T(8,128)S(1)} all-to-all(f32[8,3,2,2,4,8,128]{6,5,4,3,2,1,0:T(8,128)S(1)} %bitcast.27), channel_id=1, replica_groups=mesh['member'=8,'region'=16] {'member'}, dimensions={0} | all-to-all | bytes 3145728 | tf_op jit(solution)/shard_map/all_to_all | solution.py:252
  44.9 2.3 %shard_map.58.own_ref = f32[2,16,32,128]{3,2,1,0:T(8,128)S(1)} custom-call(f32[3072,128]{1,0:T(8,128)S(1)} %bitcast.24, f32[16,8,128]{2,1,0:T(8,128)S(1)} %all-to-all-done.1.obs_ref), custom_call_target="tpu_custom_call" | custom-call | tf_op jit(solution)/shard_map/pallas_call | solution.py:262
  47.3 3.3 %collective-permute-start = (f32[2,1,32,128]{3,2,1,0:T(8,128)S(1)}, f32[2,1,32,128]{3,2,1,0:T(8,128)S(1)}, u32[]{:S(2)}, u32[]{:S(2)}) collective-permute-start(f32[2,1,32,128]{3,2,1,0:T(8,128)S(1)} %get-tuple-element.7), channel_id=1, source_target_pairs={{0,16},{16,32},{32,48},{48,64},{64,80},{80,96},{96,112},{1,17},{17... | collective-permute-start | bytes 98312 | tf_op jit(solution)/shard_map/ppermute | solution.py:247
  50.6 1.9 %collective-permute-start.1 = (f32[2,1,32,128]{3,2,1,0:T(8,128)S(1)}, f32[2,1,32,128]{3,2,1,0:T(8,128)S(1)}, u32[]{:S(2)}, u32[]{:S(2)}) collective-permute-start(f32[2,1,32,128]{3,2,1,0:T(8,128)S(1)} %get-tuple-element.8), channel_id=1, source_target_pairs={{16,0},{32,16},{48,32},{64,48},{80,64},{96,80},{112,96},{17,1},{33... | collective-permute-start | bytes 98312 | tf_op jit(solution)/shard_map/ppermute | solution.py:247
  52.5 0.0 collective-permute-done.left_ref
  52.5 3.3 %collective-permute-done.1.right_ref = f32[2,1,32,128]{3,2,1,0:T(8,128)S(1)} collective-permute-done((f32[2,1,32,128]{3,2,1,0:T(8,128)S(1)}, f32[2,1,32,128]{3,2,1,0:T(8,128)S(1)}, u32[]{:S(2)}, u32[]{:S(2)}) %collective-permute-start.1) | collective-permute-done | bytes 32800 | tf_op jit(solution)/shard_map/ppermute | solution.py:247
  55.8 2.2 %collective-permute-start.2 = (f32[18,32,128]{2,1,0:T(8,128)S(1)}, f32[18,32,128]{2,1,0:T(8,128)S(1)}, u32[]{:S(2)}, u32[]{:S(2)}) collective-permute-start(f32[18,32,128]{2,1,0:T(8,128)S(1)} %pad_maximum_fusion), channel_id=1, source_target_pairs={{0,1},{1,2},{2,3},{3,4},{4,5},{5,6},{6,7},{7,8},{8,9},{9,10},{10,1... | collective-permute-start | bytes 884744 | tf_op jit(solution)/shard_map/ppermute | solution.py:247
  58.1 1.3 %collective-permute-start.3 = (f32[18,32,128]{2,1,0:T(8,128)S(1)}, f32[18,32,128]{2,1,0:T(8,128)S(1)}, u32[]{:S(2)}, u32[]{:S(2)}) collective-permute-start(f32[18,32,128]{2,1,0:T(8,128)S(1)} %pad_maximum_fusion.1), channel_id=1, source_target_pairs={{1,0},{2,1},{3,2},{4,3},{5,4},{6,5},{7,6},{8,7},{9,8},{10,9},{11,1... | collective-permute-start | bytes 884744 | tf_op jit(solution)/shard_map/ppermute | solution.py:247
  59.4 3.8 %collective-permute-done.2.top_ref = f32[18,32,128]{2,1,0:T(8,128)S(1)} collective-permute-done((f32[18,32,128]{2,1,0:T(8,128)S(1)}, f32[18,32,128]{2,1,0:T(8,128)S(1)}, u32[]{:S(2)}, u32[]{:S(2)}) %collective-permute-start.2) | collective-permute-done | bytes 294944 | tf_op jit(solution)/shard_map/ppermute | solution.py:247
  63.2 4.1 %collective-permute-done.3.bot_ref = f32[18,32,128]{2,1,0:T(8,128)S(1)} collective-permute-done((f32[18,32,128]{2,1,0:T(8,128)S(1)}, f32[18,32,128]{2,1,0:T(8,128)S(1)}, u32[]{:S(2)}, u32[]{:S(2)}) %collective-permute-start.3) | collective-permute-done | bytes 294944 | tf_op jit(solution)/shard_map/ppermute | solution.py:247
  67.3 17.3 %shard_map.59 = f32[3072,128]{1,0:T(8,128)S(1)} custom-call(f32[3072,128]{1,0:T(8,128)S(1)} %bitcast.25, f32[2,16,32,128]{3,2,1,0:T(8,128)S(1)} %shard_map.58.own_ref, f32[18,32,128]{2,1,0:T(8,128)S(1)} %collective-permute-done.2.top_ref, f32[18,32,128]{2,1,0:T(8,128)S(1)} %collective-permute-done.3.bot_ref, ...), custom_call_target="tpu_custom_call" | custom-call | tf_op jit(solution)/shard_map/pallas_call | solution.py:270
  84.7 24.1 %all_to_all.16 = f32[8,3,2,2,4,8,128]{6,5,4,3,2,1,0:T(8,128)S(1)} all-to-all(f32[8,3,2,2,4,8,128]{6,5,4,3,2,1,0:T(8,128)S(1)} %bitcast.26), channel_id=1, replica_groups=mesh['member'=8,'region'=16] {'member'}, dimensions={0} | all-to-all | bytes 3145728 | tf_op jit(solution)/shard_map/all_to_all | solution.py:283
  108.8 1.3 %copy.7 = f32[3,2,8,2,8,4,128]{6,4,5,3,2,1,0:T(8,128)} copy(f32[3,2,8,2,8,4,128]{6,4,5,3,1,0,2:T(8,128)S(1)} %bitcast.28) | data formatting | bytes 3145728 | tf_op jit(solution)/shard_map/transpose | solution.py:284
  (7 shorter events, 0.1 us)
Async XLA Ops:
  3.1 15.1 %all-to-all-start.1 = ((f32[16,8,128]{2,1,0:T(8,128)}), f32[16,8,128]{2,1,0:T(8,128)S(1)}, u32[]{:S(2)}, u32[]{:S(2)}) async-start(f32[16,8,128]{2,1,0:T(8,128)} %maximum_maximum_fusion), calls=%async_computation.1 | async-start | bytes 131072 | tf_op jit(solution)/shard_map/all_to_all | solution.py:260
  47.3 5.3 %collective-permute-start = (f32[2,1,32,128]{3,2,1,0:T(8,128)S(1)}, f32[2,1,32,128]{3,2,1,0:T(8,128)S(1)}, u32[]{:S(2)}, u32[]{:S(2)}) collective-permute-start(f32[2,1,32,128]{3,2,1,0:T(8,128)S(1)} %get-tuple-element.7), channel_id=1, source_target_pairs={{0,16},{16,32},{32,48},{48,64},{64,80},{80,96},{96,112},{1,17},{17... | collective-permute-start | bytes 98312 | tf_op jit(solution)/shard_map/ppermute | solution.py:247
  50.6 5.2 %collective-permute-start.1 = (f32[2,1,32,128]{3,2,1,0:T(8,128)S(1)}, f32[2,1,32,128]{3,2,1,0:T(8,128)S(1)}, u32[]{:S(2)}, u32[]{:S(2)}) collective-permute-start(f32[2,1,32,128]{3,2,1,0:T(8,128)S(1)} %get-tuple-element.8), channel_id=1, source_target_pairs={{16,0},{32,16},{48,32},{64,48},{80,64},{96,80},{112,96},{17,1},{33... | collective-permute-start | bytes 98312 | tf_op jit(solution)/shard_map/ppermute | solution.py:247
  55.8 7.3 %collective-permute-start.2 = (f32[18,32,128]{2,1,0:T(8,128)S(1)}, f32[18,32,128]{2,1,0:T(8,128)S(1)}, u32[]{:S(2)}, u32[]{:S(2)}) collective-permute-start(f32[18,32,128]{2,1,0:T(8,128)S(1)} %pad_maximum_fusion), channel_id=1, source_target_pairs={{0,1},{1,2},{2,3},{3,4},{4,5},{5,6},{6,7},{7,8},{8,9},{9,10},{10,1... | collective-permute-start | bytes 884744 | tf_op jit(solution)/shard_map/ppermute | solution.py:247
  58.1 9.2 %collective-permute-start.3 = (f32[18,32,128]{2,1,0:T(8,128)S(1)}, f32[18,32,128]{2,1,0:T(8,128)S(1)}, u32[]{:S(2)}, u32[]{:S(2)}) collective-permute-start(f32[18,32,128]{2,1,0:T(8,128)S(1)} %pad_maximum_fusion.1), channel_id=1, source_target_pairs={{1,0},{2,1},{3,2},{4,3},{5,4},{6,5},{7,6},{8,7},{9,8},{10,9},{11,1... | collective-permute-start | bytes 884744 | tf_op jit(solution)/shard_map/ppermute | solution.py:247
